TPU v7x, 32 devices: a whole 2x2x4 slice. The times are simulated.
32 devices in a mesh: dp: 4 (over x, core), fsdp: 8 (over z, y).
Axes of the slice: x: 2, y: 2, z: 4, core: 2. Of those that a mesh axis runs over, the one named last changes fastest.
Arguments:
- hidden: bfloat16 [32, 256, 4096], P(('dp', 'fsdp')), may hold values from -40 to 40
- lengths: int32 [32], P(('dp', 'fsdp')), may hold values from 64 to 256
- list_ids: int32 [32], P('dp'), may hold values from 0 to 255, as said below
- list_owner: int32 [256], replicated, may hold values from 0 to 3, as said below
- attn_gain: float32 [4096], replicated, may hold values from 0.25 to 1.75
- final_gain: float32 [4096], replicated, may hold values from 0.25 to 1.75
- w_query: bfloat16 [4096, 2048], P('fsdp'), may hold values from -24 to 24
- w_key: bfloat16 [4096, 512], P('fsdp'), may hold values from -1 to 1
- w_value: bfloat16 [4096, 512], P('fsdp'), may hold values from -0.09375 to 0.09375
- w_out: bfloat16 [2048, 4096], P('fsdp'), may hold values from -0.125 to 0.125
Outputs:
- inbox: bfloat16 [4, 4, 4, 4096], P('dp', None, None, 'fsdp')
Inputs may be any that keep to these rules, and one draw needn't show every extreme that they name: Positions from lengths[p] on are padding. `list_ids`: in each aligned block of 8 passages (those of one index of dp), at most 4 passages name lists of one owner, and in every block some owner is named by exactly 4 passages. `list_owner`: every owner holds exactly 64 lists.
All inputs are finite; a program needn't handle non-finite values.
Results may differ from a plain program's by a relative error of at most 0.0029.
The roundings to bfloat16 on the way count: a program that leaves them out, or rounds other values in their place, can miss the bound.
Values may be sent and summed in bfloat16 or wider, within the bound.
A program may use at most 64 MiB of HBM per device.

v0:
```python
import math

import jax
import jax.numpy as jnp
from jax import lax
from jax.sharding import PartitionSpec as P

HEADS = 16
KV_HEADS = 4
HEAD = 128


def rope_tables(positions, head_width):
    halfway = head_width // 2
    frequency = 10000.0 ** (-jnp.arange(halfway, dtype=jnp.float32) * 2.0 / head_width)
    angles = positions.astype(jnp.float32)[..., None] * frequency
    return (jnp.cos(angles), jnp.sin(angles))


def rotate(vectors, cosine_table, sine_table):
    halfway = vectors.shape[-1] // 2
    first_half = vectors[..., :halfway]
    second_half = vectors[..., halfway:]
    return jnp.concatenate(
        [
            first_half * cosine_table - second_half * sine_table,
            second_half * cosine_table + first_half * sine_table,
        ],
        axis=-1,
    )


def project_queries(last_normed, w_query, last_position):
    slices = lax.all_to_all(last_normed, "fsdp", split_axis=1, concat_axis=0, tiled=True)
    summed = lax.psum_scatter(
        jnp.dot(slices, w_query, preferred_element_type=jnp.float32),
        "fsdp",
        scatter_dimension=0,
        tiled=True,
    )
    shaped = summed.reshape(last_normed.shape[0], HEADS, HEAD)
    query_cos, query_sin = rope_tables(last_position, HEAD)
    rotated = rotate(shaped, query_cos[:, None, :], query_sin[:, None, :])
    return (rotated * (1.0 / math.sqrt(HEAD))).astype(jnp.bfloat16)


def attend(queries, key_rows, lengths):
    passages = queries.shape[0]
    grouped = queries.reshape(passages, KV_HEADS, HEADS // KV_HEADS, HEAD)
    scores = jnp.einsum("pkgd,ptkd->pkgt", grouped, key_rows, preferred_element_type=jnp.float32)
    visible = jnp.arange(key_rows.shape[1])[None, None, None, :] < lengths[:, None, None, None]
    scores = jnp.where(visible, scores, -jnp.inf)
    powers = jnp.exp(scores - jnp.max(scores, axis=-1, keepdims=True))
    return (powers / jnp.sum(powers, axis=-1, keepdims=True)).astype(jnp.bfloat16)


def weigh_values(weights, value_rows):
    passages = weights.shape[0]
    context = jnp.einsum(
        "pkgt,ptkd->pkgd", weights.astype(jnp.float32), value_rows, precision=lax.Precision.HIGHEST
    )
    return context.reshape(passages, HEADS * HEAD).astype(jnp.bfloat16)


def local(
    hidden, lengths, list_ids, list_owner, attn_gain, final_gain, w_query, w_key, w_value, w_out
):
    passages, seq_len, model_width = hidden.shape
    floats = hidden.astype(jnp.float32)
    normed = (
        floats * lax.rsqrt(jnp.mean(floats * floats, axis=-1, keepdims=True) + 1e-05) * attn_gain
    ).astype(jnp.bfloat16)
    flat_rows = normed.reshape(passages * seq_len, model_width)
    last_position = lengths - 1
    last_normed = jnp.take_along_axis(normed, last_position[:, None, None], axis=1)[:, 0, :]
    last_input = jnp.take_along_axis(hidden, last_position[:, None, None], axis=1)[:, 0, :].astype(
        jnp.float32
    )
    cosine_table, sine_table = rope_tables(jnp.arange(seq_len), HEAD)

    def add_rows(weight_piece):
        return jnp.dot(flat_rows, weight_piece, preferred_element_type=jnp.float32)

    key_sum = add_rows(lax.all_gather(w_key, "fsdp", axis=0, tiled=True))
    value_sum = add_rows(lax.all_gather(w_value, "fsdp", axis=0, tiled=True))
    shaped = key_sum.reshape(passages, seq_len, KV_HEADS, HEAD)
    key_rows = rotate(shaped, cosine_table[:, None, :], sine_table[:, None, :]).astype(jnp.bfloat16)
    queries = project_queries(last_normed, w_query, last_position)
    weights = attend(queries, key_rows, lengths)
    context = weigh_values(weights, value_sum.reshape(passages, seq_len, KV_HEADS, HEAD))
    context_part = lax.all_to_all(context, "fsdp", split_axis=1, concat_axis=0, tiled=True)
    mixed_out = lax.psum_scatter(
        jnp.dot(context_part, w_out, preferred_element_type=jnp.float32),
        "fsdp",
        scatter_dimension=0,
        tiled=True,
    )
    residual = last_input + mixed_out
    scaled = residual * final_gain
    embedded = (
        scaled * lax.rsqrt(jnp.mean(scaled * scaled, axis=-1, keepdims=True) + 1e-06)
    ).astype(jnp.bfloat16)
    feature_slab = lax.all_to_all(embedded, "fsdp", split_axis=1, concat_axis=0, tiled=True)
    owner_count = lax.axis_size("dp")
    capacity = max(2, 2 * lax.axis_size("fsdp") * passages // owner_count)
    list_index = jnp.arange(list_owner.shape[0])
    owners = jnp.sum(
        jnp.where(list_ids[:, None] == list_index[None, :], list_owner[None, :], 0), axis=1
    )
    owner_marks = (owners[:, None] == jnp.arange(owner_count)[None, :]).astype(jnp.int32)
    slot_rank = jnp.sum((jnp.cumsum(owner_marks, axis=0) - owner_marks) * owner_marks, axis=1)
    select = (
        (owners[None, None, :] == jnp.arange(owner_count)[:, None, None])
        & (slot_rank[None, None, :] == jnp.arange(capacity)[None, :, None])
    ).astype(jnp.bfloat16)
    outgoing = jnp.einsum(
        "osr,rd->osd", select, feature_slab, preferred_element_type=jnp.float32
    ).astype(jnp.bfloat16)
    return lax.all_to_all(outgoing[:, None], "dp", split_axis=0, concat_axis=1, tiled=True)


def solution(mesh):
    in_specs = (
        P(("dp", "fsdp"), None, None),
        P(("dp", "fsdp")),
        P("dp"),
        P(),
        P(),
        P(),
        P("fsdp", None),
        P("fsdp", None),
        P("fsdp", None),
        P("fsdp", None),
    )
    out_specs = P("dp", None, None, "fsdp")
    return jax.shard_map(local, mesh=mesh, in_specs=in_specs, out_specs=out_specs, check_vma=False)
```

profile of v0, /device:TPU:0, one launch (start us, length us, event | category | flops | bytes accessed | tf_op | source)
XLA Modules:
  0.0 364.9 jit_solution(17103655418612245779)
XLA Ops:
  7.4 2.2 fusion.1
  9.6 0.6 fusion.3
  10.3 1.3 copy-done.2
  12.2 0.7 reduce.6
  13.0 13.6 %all_to_all.57 = bf16[8,2,256]{2,1,0:T(2,128)(2,1)S(1)} all-to-all(bf16[8,2,256]{2,1,0:T(2,128)(2,1)S(1)} %reshape.360), channel_id=1, replica_groups=mesh['dp'=4,'fsdp'=8] {'fsdp'}, dimensions={0} | all-to-all | bytes 16384 | tf_op jit(solution)/shard_map/all_to_all | solution.py:34
  26.6 2.6 fusion.26
  29.3 0.7 all-gather.3.cloned.1.call-update
  30.0 0.7 all-gather.5.cloned.1.call-update
  30.8 0.7 dynamic-slice.7
  32.4 63.6 %all-reduce.5.cloned.1.call-done = f32[8,2048]{1,0:T(8,128)} async-done(((f32[8,2048]{1,0:T(8,128)}), f32[8,2048]{1,0:T(8,128)}) %all-reduce.5.cloned.1.call-update) | async-done | bytes 65552
  95.9 1.5 constant_dynamic-slice_fusion
  97.5 0.7 multiply_subtract_fusion
  98.2 72.7 %all-gather.3.cloned.1.call-done = bf16[4096,512]{1,0:T(8,128)(2,1)} async-done(((bf16[512,512]{1,0:T(8,128)(2,1)}), bf16[4096,512]{1,0:T(8,128)(2,1)}) %all-gather.3.cloned.1.call-update) | async-done | bytes 4194320 | tf_op jit(solution)/shard_map/all_gather | solution.py:84
  170.8 6.4 %copy.24 = bf16[512,4096]{1,0:T(8,128)(2,1)} copy(bf16[512,4096]{0,1:T(8,128)(2,1)} %bitcast.68) | data formatting | bytes 8388608 | tf_op jit(solution)/shard_map/dot_general | solution.py:82
  177.2 4.5 %fusion.8 = f32[1,256,4,128]{1,3,2,0:T(8,128)S(1)} fusion(bf16[4,128,4096]{2,1,0:T(8,128)(2,1)} %bitcast.71, bf16[1,256,4096]{2,1,0:T(8,128)(2,1)} %copy-done.2), kind=kOutput, calls=%fused_computation.10 | convolution fusion | flops 1073741824 | bytes 6815744 | tf_op jit(solution)/shard_map/dot_general | solution.py:82
  181.7 62.6 %all-gather.5.cloned.1.call-done = bf16[4096,512]{1,0:T(8,128)(2,1)} async-done(((bf16[512,512]{1,0:T(8,128)(2,1)}), bf16[4096,512]{1,0:T(8,128)(2,1)}) %all-gather.5.cloned.1.call-update) | async-done | bytes 4194320 | tf_op jit(solution)/shard_map/all_gather | solution.py:85
  244.3 6.5 %copy.26 = bf16[512,4096]{1,0:T(8,128)(2,1)} copy(bf16[512,4096]{0,1:T(8,128)(2,1)} %bitcast.69) | data formatting | bytes 8388608 | tf_op jit(solution)/shard_map/dot_general | solution.py:82
  250.8 4.1 %fusion.4 = f32[256,4,128]{2,0,1:T(8,128)S(1)} fusion(bf16[4,128,4096]{2,1,0:T(8,128)(2,1)} %bitcast.70, bf16[1,256,4096]{2,1,0:T(8,128)(2,1)} %copy-done.2), kind=kOutput, calls=%fused_computation.6 | convolution fusion | flops 1073741824 | bytes 6815744 | tf_op jit(solution)/shard_map/dot_general | solution.py:82
  255.0 1.1 fusion.58
  256.4 0.7 reduce.7
  257.7 3.3 all-to-all-start.1
  261.1 0.9 select_reduce_fusion
  262.0 5.4 %all-to-all-done.1 = bf16[8,2,128]{2,1,0:T(2,128)(2,1)S(1)} async-done(((bf16[8,2,128]{2,1,0:T(2,128)(2,1)}), bf16[8,2,128]{2,1,0:T(2,128)(2,1)S(1)}, u32[]{:S(2)}, u32[]{:S(2)}) %all-to-all-start.1) | async-done | bytes 4128 | tf_op jit(solution)/shard_map/all_to_all | solution.py:91
  267.4 1.0 fusion.32
  268.7 68.0 %all-reduce.7.cloned.1.call-done = f32[8,4096]{1,0:T(8,128)} async-done(((f32[8,4096]{1,0:T(8,128)}), f32[8,4096]{1,0:T(8,128)}) %all-reduce.7.cloned.1.call-update) | async-done | bytes 131088
  336.7 2.3 multiply_reduce_fusion
  339.6 0.7 reduce.8
  340.4 0.6 reshape.364
  341.0 3.7 %all-to-all-start.2 = ((bf16[8,2,256]{2,1,0:T(2,128)(2,1)}), bf16[8,2,256]{2,1,0:T(2,128)(2,1)S(1)}, u32[]{:S(2)}, u32[]{:S(2)}) async-start(bf16[8,2,256]{2,1,0:T(2,128)(2,1)} %reshape.364), calls=%async_computation.2 | async-start | bytes 16384 | tf_op jit(solution)/shard_map/all_to_all | solution.py:103
  344.7 6.5 %all-to-all-done.2 = bf16[8,2,256]{2,1,0:T(2,128)(2,1)S(1)} async-done(((bf16[8,2,256]{2,1,0:T(2,128)(2,1)}), bf16[8,2,256]{2,1,0:T(2,128)(2,1)S(1)}, u32[]{:S(2)}, u32[]{:S(2)}) %all-to-all-start.2) | async-done | bytes 8224 | tf_op jit(solution)/shard_map/all_to_all | solution.py:103
  351.4 6.4 %all_to_all.58 = bf16[4,1,4,512]{3,2,1,0:T(4,128)(2,1)S(1)} all-to-all(bf16[4,1,4,512]{3,2,1,0:T(4,128)(2,1)S(1)} %fusion.12), channel_id=1, replica_groups=mesh['dp'=4,'fsdp'=8] {'dp'}, dimensions={0} | all-to-all | bytes 32768 | tf_op jit(solution)/shard_map/all_to_all | solution.py:119
  357.7 0.6 copy.50
  (39 shorter events, 3.2 us)
Async XLA Ops:
  6.5 260.9 %copy-start = (bf16[256,4096]{1,0:T(8,128)(2,1)S(1)}, bf16[256,4096]{1,0:T(8,128)(2,1)}, u32[]{:S(2)}) copy-start(bf16[256,4096]{1,0:T(8,128)(2,1)} %param.21) | copy-start | bytes 6291460
  6.5 3.0 copy-start.3
  6.5 89.4 %all-reduce.5.cloned.1.call-start = ((), (), s32[]{:S(2)}) async-start(), calls=%async_computation.6 | async-start | bytes 131072
  6.5 3.0 copy-start.1
  10.2 1.4 copy-start.2
  10.2 20.5 %copy-start.5 = (u32[32]{0:T(128)S(1)}, u32[32]{0:T(128)}, u32[]{:S(2)}) copy-start(u32[32]{0:T(128)} %constant.78) | copy-start | bytes 388
  29.2 141.6 %all-gather.3.cloned.1.call-start = ((), (), s32[]{:S(2)}) async-start(), calls=%async_computation.4 | async-start | bytes 4718592 | tf_op jit(solution)/shard_map/all_gather | solution.py:84
  30.0 214.3 %all-gather.5.cloned.1.call-start = ((), (), s32[]{:S(2)}) async-start(), calls=%async_computation.5 | async-start | bytes 4718592 | tf_op jit(solution)/shard_map/all_gather | solution.py:85
  254.9 81.8 %copy-start.4 = (f32[4096]{0:T(1024)S(1)}, f32[4096]{0:T(1024)}, u32[]{:S(2)}) copy-start(f32[4096]{0:T(1024)} %param.17) | copy-start | bytes 49156
  257.7 9.7 %all-to-all-start.1 = ((bf16[8,2,128]{2,1,0:T(2,128)(2,1)}), bf16[8,2,128]{2,1,0:T(2,128)(2,1)S(1)}, u32[]{:S(2)}, u32[]{:S(2)}) async-start(bf16[8,2,128]{2,1,0:T(2,128)(2,1)} %reshape.362), calls=%async_computation.1 | async-start | bytes 8192 | tf_op jit(solution)/shard_map/all_to_all | solution.py:91
  261.0 75.6 %all-reduce.7.cloned.1.call-start = ((), (), s32[]{:S(2)}) async-start(), calls=%async_computation.7 | async-start | bytes 262144
  341.0 10.2 %all-to-all-start.2 = ((bf16[8,2,256]{2,1,0:T(2,128)(2,1)}), bf16[8,2,256]{2,1,0:T(2,128)(2,1)S(1)}, u32[]{:S(2)}, u32[]{:S(2)}) async-start(bf16[8,2,256]{2,1,0:T(2,128)(2,1)} %reshape.364), calls=%async_computation.2 | async-start | bytes 16384 | tf_op jit(solution)/shard_map/all_to_all | solution.py:103
Sparse Core Ops, SparseCore 0:
  29.4 66.5 all-reduce.4
  98.1 72.7 all-gather.2
  173.0 71.3 all-gather.4
  268.6 68.0 all-reduce.6
where the time goes:
time: 366 us; the launch traced here: 365 us
  waiting for transfers between devices  280 us (77%)
  blocking collectives  20 us (5%)
  local copies, waits for them, and re-layouts  18.9 us (5%)
  between operations  14.8 us (4%)
  matrix products  13.7 us (4%)
  other arithmetic  10.1 us (3%)
  starting transfers between devices  7.14 us (2%)
    unnamed x6, waiting for transfers between devices  133 us
    all_gather x1, waiting for transfers between devices, local(): key_sum = add_rows(lax.all_gather(w_key, 'fsdp', axis=0, tiled=True))  72.7 us
    all_gather x1, waiting for transfers between devices, local(): value_sum = add_rows(lax.all_gather(w_value, 'fsdp', axis=0, tiled=True))  62.6 us
    all_to_all x1, blocking collectives, project_queries(): lax.all_to_all(last_normed, 'fsdp', split_axis=1, concat_axis=0, tiled=True)  13.6 us
    dot_general x2, local copies, waits for them, and re-layouts, add_rows(): return jnp.dot(flat_rows, weight_piece, preferred_element_type=jnp.float32)  12.8 us
    dot_general x2, matrix products, add_rows(): return jnp.dot(flat_rows, weight_piece, preferred_element_type=jnp.float32)  8.56 us
  transfers between devices with their start and end apart: 6, of which 6 were waited for; matrix products, arithmetic and copies ran while one was open for 4% of the time, Pallas kernels for 0%

commit v1 on v0

v1 whole, which is shorter than its diff:
```python
import functools
import math

import jax
import jax.numpy as jnp
import numpy as np
from jax import lax
from jax.experimental import pallas as pl
from jax.experimental.pallas import tpu as pltpu
from jax.sharding import PartitionSpec as P

HEADS = 16
KV_HEADS = 4
HEAD = 128
GROUP = HEADS // KV_HEADS
MESH = pl.DeviceIdType.MESH
F32 = jnp.float32
BF16 = jnp.bfloat16


def rope_tables(seq_len):
    half = HEAD // 2
    exponent = -np.arange(half, dtype=np.float32) * np.float32(2.0) / np.float32(HEAD)
    frequency = (np.float64(10000.0) ** exponent.astype(np.float64)).astype(np.float32)
    angles = (np.arange(seq_len, dtype=np.float32)[:, None] * frequency).astype(np.float64)
    cosine, sine = np.cos(angles), np.sin(angles)
    return (
        np.concatenate([cosine, cosine], axis=1).astype(np.float32),
        np.concatenate([-sine, sine], axis=1).astype(np.float32),
    )


def kernel(
    n_dp, n, chunks,
    lengths, list_ids,
    owners_hbm, hidden_hbm, again_hbm, fgain_hbm, cos_hbm, sin_hbm, wq_hbm, wk_hbm, wv_hbm, wo_hbm,
    out_ref,
    hid, normed, again, fgain, cos_t, sin_t, wq, wk, wv, wo,
    owners, acc, last_in, gain2,
    x_send, x_recv, q_send, q_recv, u_send, u_recv, mixed, c_send, c_recv, o_send, o_recv,
    e_send, e_recv,
    load_sem, a2a_send, a2a_recv,
    zu_s, zd_s, y_s, x_s, dz_s, dy_s, dx_s, z_r, y_r, x_r, dz_r, dy_r, dx_r,
):
    dp = lax.axis_index("dp")
    f = lax.axis_index("fsdp")
    seq_len, width = hid.shape
    slab = width // n
    depth = n // 2
    total = n_dp * n
    cap = out_ref.shape[2]
    a, b = f // 2, f % 2
    core, x_bit = dp % 2, (dp // 2) % 2
    partner = dp + 1 - 2 * core
    x_peer = dp + 2 - 4 * x_bit

    sources = (wk_hbm, hidden_hbm.at[0], again_hbm, wq_hbm, cos_hbm, sin_hbm, wv_hbm, wo_hbm, fgain_hbm,
               owners_hbm)
    targets = (wk.at[f], hid, again, wq, cos_t, sin_t, wv, wo, fgain, owners)
    loads = [
        pltpu.make_async_copy(s, t, load_sem.at[i])
        for i, (s, t) in enumerate(zip(sources, targets))
    ]
    for load in loads:
        load.start()

    me = dp * n + f
    barrier = pltpu.get_barrier_semaphore()

    def greet(t, carry):
        other = lax.rem(me + t, total)
        pl.semaphore_signal(
            barrier, inc=1, device_id=(other // n, other % n), device_id_type=MESH
        )
        return carry

    lax.fori_loop(1, total, greet, 0)
    pl.semaphore_wait(barrier, total - 1)

    step = slab // chunks

    def piece(pa, pb, offset, rows, send_sem, recv_sem, device):
        part = wk.at[pa * 2 + pb, pl.ds(pl.multiple_of(offset, rows), rows), :]
        return pltpu.make_async_remote_copy(
            src_ref=part, dst_ref=part, send_sem=send_sem, recv_sem=recv_sem,
            device_id=device, device_id_type=MESH,
        )

    def half_at(k, c):
        return k * step + c * (step // 2)

    def quarter_at(k, c, x):
        return half_at(k, c) + x * (step // 4)

    half, quarter = step // 2, step // 4

    def up(pa, k):
        return piece(pa, b, half_at(k, core), half, zu_s.at[pa, k], z_r.at[pa, k], (dp, lax.rem(f + 2, n)))

    def down(pa, k):
        return piece(pa, b, half_at(k, core), half, zd_s.at[pa, k], z_r.at[pa, k], (dp, lax.rem(f + n - 2, n)))

    def cross_y(pa, pb, k):
        return piece(pa, pb, quarter_at(k, core, x_bit), quarter, y_s.at[pa, k], y_r.at[pa, k], (dp, 2 * a + 1 - b))

    def cross_x(pa, k, x):
        return piece(pa, 1 - b, quarter_at(k, core, x), quarter, x_s.at[pa, k], x_r.at[pa, k], (x_peer, f))

    def core_z(pa, k, c):
        return piece(pa, b, half_at(k, c), half, dz_s.at[pa, k], dz_r.at[pa, k], (partner, f))

    def core_y(pa, k, c):
        return piece(pa, 1 - b, quarter_at(k, c, x_bit), quarter, dy_s.at[pa, k], dy_r.at[pa, k], (partner, f))

    def core_x(pa, k, c):
        return piece(pa, 1 - b, quarter_at(k, c, 1 - x_bit), quarter, dx_s.at[pa, k], dx_r.at[pa, k], (partner, f))

    loads[0].wait()
    for k in range(chunks):
        @pl.when(a < depth - 1)
        def _():
            up(a, k).start()

        @pl.when(a > 0)
        def _():
            down(a, k).start()

        cross_y(a, b, k).start()

    def exchange(slot, send, recv):
        def one(t, carry):
            g = lax.rem(f + t, n)
            pltpu.make_async_remote_copy(
                src_ref=send.at[g], dst_ref=recv.at[f], send_sem=a2a_send.at[slot],
                recv_sem=a2a_recv.at[slot], device_id=(dp, g), device_id_type=MESH,
            ).start()
            return carry

        lax.fori_loop(1, n, one, 0)
        recv[f] = send[f]

    def arrived(slot, recv, count):
        blocks = recv.at[pl.ds(0, count)]
        pltpu.make_async_copy(blocks, blocks, a2a_recv.at[slot]).wait()

    def sent(slot, recv, count):
        blocks = recv.at[pl.ds(0, count)]
        pltpu.make_async_copy(blocks, blocks, a2a_send.at[slot]).wait()

    loads[1].wait()
    loads[2].wait()
    last = lengths[0] - 1
    picks = lax.broadcasted_iota(jnp.int32, (16, seq_len), 1) == last
    picks = jnp.where(picks, 1.0, 0.0).astype(BF16)
    row = jnp.concatenate(
        [
            jnp.dot(picks, hid[:, g * slab:(g + 1) * slab], preferred_element_type=F32)[:1]
            for g in range(n)
        ],
        axis=1,
    )
    scale = lax.rsqrt(jnp.mean(row * row, axis=-1, keepdims=True) + 1e-05)
    row_normed = (row * scale * again[...]).astype(BF16).astype(F32)
    for g in range(n):
        x_send[g] = row_normed[:, g * slab:(g + 1) * slab]
        last_in[g:g + 1, :] = row[:, g * slab:(g + 1) * slab]
    exchange(0, x_send, x_recv)

    block = 16

    def normalise(i, carry):
        window = pl.ds(pl.multiple_of(i * block, block), block)
        x = hid[window, :].astype(F32)
        r = lax.rsqrt(jnp.mean(x * x, axis=-1, keepdims=True) + 1e-05)
        normed[window, :] = (x * r * again[...]).astype(BF16)
        return carry

    lax.fori_loop(0, seq_len // block, normalise, 0)

    loads[3].wait()
    arrived(0, x_recv, n - 1)
    x_all = jnp.concatenate([x_recv[i] for i in range(n)], axis=0).astype(BF16)
    for h in range(HEADS):
        q_send[:, h, :] = jnp.dot(
            x_all, wq[:, h * HEAD:(h + 1) * HEAD], preferred_element_type=F32
        )
    exchange(1, q_send, q_recv)

    acc[...] = jnp.zeros_like(acc)

    def accumulate(slab_index):
        columns = pl.ds(pl.multiple_of(slab_index * slab, slab), slab)
        acc[...] += jnp.dot(normed[:, columns], wk[slab_index], preferred_element_type=F32)

    accumulate(f)

    def around(e, body):
        for sign in (1, -1):
            pa = a + sign * e
            valid = (pa >= 0) & (pa < depth) & (e >= (0 if sign == 1 else 1))

            @pl.when(valid)
            def _():
                body(pa, sign)

    def gather_step(d, carry):
        def from_z(pa, sign):
            for k in range(chunks):
                up(pa, k).wait_recv()
                if sign == 1:
                    @pl.when(a > 0)
                    def _():
                        down(pa, k).start()
                else:
                    @pl.when(a < depth - 1)
                    def _():
                        up(pa, k).start()
                cross_y(pa, b, k).start()
                core_z(pa, k, core).start()

        def from_y(pa, sign):
            for k in range(chunks):
                cross_y(pa, 1 - b, k).wait_recv()
                cross_x(pa, k, x_bit).start()
                core_y(pa, k, core).start()

        def from_x(pa, sign):
            for k in range(chunks):
                cross_x(pa, k, 1 - x_bit).wait_recv()
                core_x(pa, k, core).start()

        def consume(pa, sign):
            @pl.when(pa != a)
            def _():
                for k in range(chunks):
                    core_z(pa, k, 1 - core).wait_recv()
                accumulate(pa * 2 + b)

            for k in range(chunks):
                core_y(pa, k, 1 - core).wait_recv()
                core_x(pa, k, 1 - core).wait_recv()
            accumulate(pa * 2 + 1 - b)

        @pl.when(d >= 1)
        def _():
            around(d, from_z)
            around(d - 1, from_y)
            around(d - 1, from_x)

        @pl.when(d >= 2)
        def _():
            around(d - 2, consume)

        return carry

    lax.fori_loop(1, depth + 2, gather_step, 0)

    for load in loads[4:]:
        load.wait()
    arrived(1, q_recv, n - 1)
    queries = jnp.sum(q_recv[...], axis=0)
    at_last = lax.broadcasted_iota(jnp.int32, cos_t.shape, 0) == last
    q_cos = jnp.sum(jnp.where(at_last, cos_t[...], 0.0), axis=0, keepdims=True)
    q_sin = jnp.sum(jnp.where(at_last, sin_t[...], 0.0), axis=0, keepdims=True)
    queries = queries * q_cos + pltpu.roll(queries, HEAD // 2, 1) * q_sin
    queries = (queries * (1.0 / math.sqrt(HEAD))).astype(BF16)

    scores = jnp.zeros((HEADS, seq_len), F32)
    head_of = lax.broadcasted_iota(jnp.int32, scores.shape, 0) // GROUP
    for kv in range(KV_HEADS):
        keys = acc[:, kv * HEAD:(kv + 1) * HEAD]
        keys = (keys * cos_t[...] + pltpu.roll(keys, HEAD // 2, 1) * sin_t[...]).astype(BF16)
        part = lax.dot_general(queries, keys, (((1,), (1,)), ((), ())), preferred_element_type=F32)
        scores = jnp.where(head_of == kv, part, scores)
    visible = lax.broadcasted_iota(jnp.int32, scores.shape, 1) < lengths[0]
    scores = jnp.where(visible, scores, -jnp.inf)
    powers = jnp.exp(scores - jnp.max(scores, axis=-1, keepdims=True))
    weights = (powers / jnp.sum(powers, axis=-1, keepdims=True)).astype(BF16)

    for g in range(n):
        u_send[g] = jnp.dot(weights, normed[:, g * slab:(g + 1) * slab], preferred_element_type=F32)
    exchange(2, u_send, u_recv)
    arrived(2, u_recv, n - 1)
    sums = u_recv[...].reshape(n * HEADS, slab)
    top = sums.astype(BF16)
    rest = sums - top.astype(F32)
    middle = rest.astype(BF16)
    low = (rest - middle.astype(F32)).astype(BF16)
    values = wv[...]
    product = (
        jnp.dot(low, values, preferred_element_type=F32)
        + jnp.dot(middle, values, preferred_element_type=F32)
    ) + jnp.dot(top, values, preferred_element_type=F32)
    for kv in range(KV_HEADS):
        mixed[kv] = product[:, kv * HEAD:(kv + 1) * HEAD]

    share = HEADS * HEAD // n
    for h in range(HEADS):
        kv = h // GROUP
        part = mixed[kv, pl.ds(h, n, stride=HEADS), :]
        if share >= HEAD:
            at = h * HEAD % share
            c_send[h * HEAD // share, :, at:at + HEAD] = part
        else:
            pieces = HEAD // share
            for i in range(pieces):
                c_send[h * pieces + i] = part[:, i * share:(i + 1) * share]
    exchange(3, c_send, c_recv)
    arrived(3, c_recv, n - 1)
    context = jnp.sum(c_recv[...], axis=0).astype(BF16)
    for g in range(n):
        o_send[:, g, :] = jnp.dot(
            context, wo[:, g * slab:(g + 1) * slab], preferred_element_type=F32
        )
        gain2[g:g + 1, :] = fgain[:, g * slab:(g + 1) * slab]
    exchange(4, o_send, o_recv)

    lists = lax.broadcasted_iota(jnp.int32, owners.shape, 1)

    def owner_of(r):
        held = jnp.where(lists == list_ids[r], owners[...], 0)
        return jnp.sum(held.astype(F32), axis=1, keepdims=True)

    owner = owner_of(f)

    def count(r, slot):
        same = jnp.where(owner_of(r) == owner, 1.0, 0.0)
        return slot + same * jnp.where(r < f, 1.0, 0.0)

    code = owner * cap + lax.fori_loop(0, n, count, jnp.zeros((1, 1), F32))

    arrived(4, o_recv, n - 1)
    scaled = (last_in[...] + jnp.sum(o_recv[...], axis=0)) * gain2[...]
    square = jnp.sum(jnp.sum(scaled * scaled, axis=1, keepdims=True), axis=0, keepdims=True)
    embedded = (scaled * lax.rsqrt(square / width + 1e-06)).astype(BF16).astype(F32)
    for g in range(n):
        e_send[g, :, :slab] = embedded[g:g + 1, :]
        e_send[g, :, slab:] = jnp.broadcast_to(code, (1, 128))

    def post(t, carry):
        other = lax.rem(me + t, total)
        g = other % n
        pltpu.make_async_remote_copy(
            src_ref=e_send.at[g], dst_ref=e_recv.at[me], send_sem=a2a_send.at[5],
            recv_sem=a2a_recv.at[5], device_id=(other // n, g), device_id_type=MESH,
        ).start()
        return carry

    lax.fori_loop(1, total, post, 0)
    e_recv[me] = e_send[f]
    arrived(5, e_recv, total - 1)

    first = (dp * cap).astype(F32)
    for j in range(n_dp):
        rows = jnp.concatenate([e_recv[j * n + i] for i in range(n)], axis=0)
        codes = rows[:, slab:slab + 1]
        for s in range(cap):
            kept = jnp.where(codes == first + s, rows[:, :slab], 0.0)
            out_ref[0, j, s:s + 1, :] = jnp.sum(kept, axis=0, keepdims=True).astype(BF16)

    for index, recv in ((0, x_recv), (1, q_recv), (2, u_recv), (3, c_recv), (4, o_recv)):
        sent(index, recv, n - 1)
    sent(5, e_recv, total - 1)

    def drain(pa, carry):
        for k in range(chunks):
            @pl.when((pa <= a) & (a < depth - 1))
            def _():
                up(pa, k).wait_send()

            @pl.when((pa >= a) & (a > 0))
            def _():
                down(pa, k).wait_send()

            @pl.when(pa != a)
            def _():
                core_z(pa, k, core).wait_send()

            cross_y(pa, b, k).wait_send()
            cross_x(pa, k, x_bit).wait_send()
            core_y(pa, k, core).wait_send()
            core_x(pa, k, core).wait_send()
        return carry

    lax.fori_loop(0, depth, drain, 0)


def local(
    n_dp, n,
    hidden, lengths, list_ids, list_owner, attn_gain, final_gain, w_query, w_key, w_value, w_out,
):
    _, seq_len, width = hidden.shape
    slab = width // n
    depth = n // 2
    chunks = 2 if n <= 8 else 1
    cap = max(2, 2 * n // n_dp)
    share = HEADS * HEAD // n
    cosine, sine = rope_tables(seq_len)
    pieces = pltpu.SemaphoreType.DMA((depth, chunks))
    any_spec = pl.BlockSpec(memory_space=pl.ANY)
    smem_spec = pl.BlockSpec(memory_space=pltpu.SMEM)
    vmem = pltpu.VMEM
    return pl.pallas_call(
        functools.partial(kernel, n_dp, n, chunks),
        out_shape=jax.ShapeDtypeStruct((1, n_dp, cap, slab), BF16),
        in_specs=[smem_spec] * 2 + [any_spec] * 10,
        out_specs=pl.BlockSpec(memory_space=pltpu.VMEM),
        scratch_shapes=[
            vmem((seq_len, width), BF16),
            vmem((seq_len, width), BF16),
            vmem((1, width), F32),
            vmem((1, width), F32),
            vmem((seq_len, HEAD), F32),
            vmem((seq_len, HEAD), F32),
            vmem(w_query.shape, BF16),
            vmem((n,) + w_key.shape, BF16),
            vmem(w_value.shape, BF16),
            vmem(w_out.shape, BF16),
            vmem((1, list_owner.shape[0]), jnp.int32),
            vmem((seq_len, KV_HEADS * HEAD), F32),
            vmem((n, slab), F32),
            vmem((n, slab), F32),
            vmem((n, 1, slab), F32),
            vmem((n, 1, slab), F32),
            vmem((n, HEADS, HEAD), F32),
            vmem((n, HEADS, HEAD), F32),
            vmem((n, HEADS, slab), F32),
            vmem((n, HEADS, slab), F32),
            vmem((KV_HEADS, n * HEADS, HEAD), F32),
            vmem((n, n, share), F32),
            vmem((n, n, share), F32),
            vmem((n, n, slab), F32),
            vmem((n, n, slab), F32),
            vmem((n, 1, slab + 128), F32),
            vmem((n_dp * n, 1, slab + 128), F32),
            pltpu.SemaphoreType.DMA((10,)),
            pltpu.SemaphoreType.DMA((6,)),
            pltpu.SemaphoreType.DMA((6,)),
        ] + [pieces] * 13,
        compiler_params=pltpu.CompilerParams(
            collective_id=0, has_side_effects=True, vmem_limit_bytes=67043328
        ),
    )(
        lengths, list_ids,
        list_owner.reshape(1, -1), hidden, attn_gain.reshape(1, width), final_gain.reshape(1, width),
        cosine, sine, w_query, w_key, w_value, w_out,
    )


def solution(mesh):
    in_specs = (
        P(("dp", "fsdp"), None, None),
        P(("dp", "fsdp")),
        P("dp"),
        P(),
        P(),
        P(),
        P("fsdp", None),
        P("fsdp", None),
        P("fsdp", None),
        P("fsdp", None),
    )
    out_specs = P("dp", None, None, "fsdp")
    body = functools.partial(local, mesh.shape["dp"], mesh.shape["fsdp"])
    return jax.shard_map(body, mesh=mesh, in_specs=in_specs, out_specs=out_specs, check_vma=False)
```

time: 366 us -> 68.8 us (0.19)
  waiting for transfers between devices: 280 us -> 0 us
  Pallas kernels: 0 us -> 66.5 us
  blocking collectives: 20 us -> 0 us
  local copies, waits for them, and re-layouts: 18.9 us -> 1.33 us
  between operations: 14.8 us -> 0.66 us
  matrix products: 13.7 us -> 0 us
  other arithmetic: 10.1 us -> 0 us
  starting transfers between devices: 7.14 us -> 0 us
    all_gather x2 -> x0, waiting for transfers between devices: 135 us -> none  [the longest x1 72.7 us: local(): key_sum = add_rows(lax.all_gather(w_key, 'fsdp', axis=0, tiled=True))]
    unnamed x6 -> x0, waiting for transfers between devices: 133 us -> none
    pallas_call x0 -> x1, Pallas kernels: none -> 66.5 us  [local(): pl.pallas_call(functools.partial(kernel, n_dp, n, chunks), out_shape=jax....]
    all_to_all x2 -> x0, blocking collectives: 20 us -> none  [the longest x1 13.6 us: project_queries(): lax.all_to_all(last_normed, 'fsdp', split_axis=1, concat_axis=0, tiled=True)]
    dot_general x2 -> x0, local copies, waits for them, and re-layouts: 12.8 us -> none  [add_rows(): return jnp.dot(flat_rows, weight_piece, preferred_element_type=jnp.float32)]
    dot_general x6 -> x0, matrix products: 12.6 us -> none  [the longest x2 8.56 us: add_rows(): return jnp.dot(flat_rows, weight_piece, preferred_element_type=jnp.float32)]
    all_to_all x2 -> x0, waiting for transfers between devices: 12 us -> none  [the longest x1 6.51 us: local(): lax.all_to_all(embedded, 'fsdp', split_axis=1, concat_axis=0, tiled=True)]
    all_to_all x2 -> x0, starting transfers between devices: 7.01 us -> none  [the longest x1 3.7 us: local(): lax.all_to_all(embedded, 'fsdp', split_axis=1, concat_axis=0, tiled=True)]
  transfers between devices with their start and end apart: 6 -> 0, of which waited for: 6 -> 0; matrix products, arithmetic and copies ran while one was open for 4% -> 0% of each run, Pallas kernels for 0% -> 0%
where the time goes in v1:
time: 68.8 us; the launch traced here: 68.5 us
  Pallas kernels  66.5 us (97%)
  local copies, waits for them, and re-layouts  1.33 us (2%)
    pallas_call x1, Pallas kernels, local(): pl.pallas_call(functools.partial(kernel, n_dp, n, chunks), out_shape=jax....  66.5 us

profile of v1, /device:TPU:0, one launch (start us, length us, event | category | flops | bytes accessed | tf_op | source)
XLA Modules:
  0.0 68.5 jit_solution(1987132406583927535)
XLA Ops:
  0.7 66.5 %shard_map.118 = bf16[1,4,4,512]{3,2,1,0:T(4,128)(2,1)} custom-call(s32[1]{0:T(128)S(6)} %copy.14.lengths, s32[8]{0:T(128)} %list_ids.1, s32[1,256]{1,0:T(1,128)} %bitcast.5, bf16[1,256,4096]{2,1,0:T(8,128)(2,1)} %hidden_hbm.1, f32[1,4096]{1,0:T(1,128)} %bitcast.3, f32[1,4096]{1,0:T(1,128)} %bitcast.4, f32[256,128]{1,0:T(8,128)} %constant.4.clone.cos_hbm, ...), custom_call_target="tpu_custom_call" | custom-call | tf_op jit(solution)/shard_map/pallas_call | solution.py:403
  67.2 1.3 %copy.15 = bf16[1,4,4,512]{3,2,1,0:T(4,128)(2,1)} copy(bf16[1,4,4,512]{3,2,1,0:T(4,128)(2,1)} %shard_map.118) | data formatting | bytes 32768

commit v2 on v1

--- a/solution.py
+++ b/solution.py
@@ -39,7 +39,7 @@
     owners, acc, last_in, gain2,
     x_send, x_recv, q_send, q_recv, u_send, u_recv, mixed, c_send, c_recv, o_send, o_recv,
     e_send, e_recv,
-    load_sem, a2a_send, a2a_recv,
+    load_sem, a2a_send, a2a_recv, round_sem,
     zu_s, zd_s, y_s, x_s, dz_s, dy_s, dx_s, z_r, y_r, x_r, dz_r, dy_r, dx_r,
 ):
     dp = lax.axis_index("dp")
@@ -65,17 +65,51 @@
         load.start()
 
     me = dp * n + f
+
+    def wrap(index, size):
+        return jnp.where(index >= size, index - size, index)
+
+    def each(low, high, body):
+        if high <= 8:
+            for t in range(low, high):
+                body(t)
+        else:
+            lax.fori_loop(low, high, lambda t, c: (body(t), c)[1], 0)
+
+    def everyone(body):
+        for t in range(n_dp):
+            o = wrap(dp + t, n_dp)
+            each(1 if t == 0 else 0, n, lambda i: body(o, wrap(f + i, n)))
+
     barrier = pltpu.get_barrier_semaphore()
 
-    def greet(t, carry):
-        other = lax.rem(me + t, total)
-        pl.semaphore_signal(
-            barrier, inc=1, device_id=(other // n, other % n), device_id_type=MESH
-        )
-        return carry
-
-    lax.fori_loop(1, total, greet, 0)
-    pl.semaphore_wait(barrier, total - 1)
+    def flip(index, bit):
+        return index + bit * (1 - 2 * ((index // bit) % 2))
+
+    peers = [(flip(dp, 1 << i), f) for i in range((n_dp - 1).bit_length())]
+    peers += [(dp, flip(f, 1 << i)) for i in range((n - 1).bit_length())]
+
+    def greet(o, g):
+        pl.semaphore_signal(barrier, inc=1, device_id=(o, g), device_id_type=MESH)
+
+    for o, g in peers:
+        greet(o, g)
+
+    @pl.when(a < depth - 1)
+    def _():
+        greet(dp, f + 2)
+
+    @pl.when(a > 0)
+    def _():
+        greet(dp, f - 2)
+
+    inner = jnp.where((a > 0) & (a < depth - 1), 1, 0)
+    pl.semaphore_wait(barrier, len(peers) + 1 + inner)
+
+    def greet_all():
+        for i, (o, g) in enumerate(peers):
+            pl.semaphore_signal(round_sem.at[i], inc=1, device_id=(o, g), device_id_type=MESH)
+            pl.semaphore_wait(round_sem.at[i], 1)
 
     step = slab // chunks
 
@@ -127,16 +161,14 @@
 
         cross_y(a, b, k).start()
 
+    def give(slot, send, recv, g):
+        pltpu.make_async_remote_copy(
+            src_ref=send.at[g], dst_ref=recv.at[f], send_sem=a2a_send.at[slot],
+            recv_sem=a2a_recv.at[slot], device_id=(dp, g), device_id_type=MESH,
+        ).start()
+
     def exchange(slot, send, recv):
-        def one(t, carry):
-            g = lax.rem(f + t, n)
-            pltpu.make_async_remote_copy(
-                src_ref=send.at[g], dst_ref=recv.at[f], send_sem=a2a_send.at[slot],
-                recv_sem=a2a_recv.at[slot], device_id=(dp, g), device_id_type=MESH,
-            ).start()
-            return carry
-
-        lax.fori_loop(1, n, one, 0)
+        each(1, n, lambda t: give(slot, send, recv, wrap(f + t, n)))
         recv[f] = send[f]
 
     def arrived(slot, recv, count):
@@ -164,6 +196,7 @@
     for g in range(n):
         x_send[g] = row_normed[:, g * slab:(g + 1) * slab]
         last_in[g:g + 1, :] = row[:, g * slab:(g + 1) * slab]
+    greet_all()
     exchange(0, x_send, x_recv)
 
     block = 16
@@ -177,14 +210,15 @@
 
     lax.fori_loop(0, seq_len // block, normalise, 0)
 
-    loads[3].wait()
-    arrived(0, x_recv, n - 1)
-    x_all = jnp.concatenate([x_recv[i] for i in range(n)], axis=0).astype(BF16)
-    for h in range(HEADS):
-        q_send[:, h, :] = jnp.dot(
-            x_all, wq[:, h * HEAD:(h + 1) * HEAD], preferred_element_type=F32
-        )
-    exchange(1, q_send, q_recv)
+    def partial_queries():
+        loads[3].wait()
+        arrived(0, x_recv, n - 1)
+        x_all = jnp.concatenate([x_recv[i] for i in range(n)], axis=0).astype(BF16)
+        for h in range(HEADS):
+            q_send[:, h, :] = jnp.dot(
+                x_all, wq[:, h * HEAD:(h + 1) * HEAD], preferred_element_type=F32
+            )
+        exchange(1, q_send, q_recv)
 
     acc[...] = jnp.zeros_like(acc)
 
@@ -245,15 +279,22 @@
         def _():
             around(d, from_z)
             around(d - 1, from_y)
-            around(d - 1, from_x)
 
         @pl.when(d >= 2)
         def _():
-            around(d - 2, consume)
+            around(d - 2, from_x)
+
+        @pl.when(d == 2)
+        def _():
+            partial_queries()
+
+        @pl.when(d >= 3)
+        def _():
+            around(d - 3, consume)
 
         return carry
 
-    lax.fori_loop(1, depth + 2, gather_step, 0)
+    lax.fori_loop(1, depth + 3, gather_step, 0)
 
     for load in loads[4:]:
         load.wait()
@@ -277,9 +318,15 @@
     powers = jnp.exp(scores - jnp.max(scores, axis=-1, keepdims=True))
     weights = (powers / jnp.sum(powers, axis=-1, keepdims=True)).astype(BF16)
 
-    for g in range(n):
-        u_send[g] = jnp.dot(weights, normed[:, g * slab:(g + 1) * slab], preferred_element_type=F32)
-    exchange(2, u_send, u_recv)
+    def weighted(g):
+        columns = pl.ds(pl.multiple_of(g * slab, slab), slab)
+        return jnp.dot(weights, normed[:, columns], preferred_element_type=F32)
+
+    for t in range(1, n):
+        g = wrap(f + t, n)
+        u_send[g] = weighted(g)
+        give(2, u_send, u_recv, g)
+    u_recv[f] = weighted(f)
     arrived(2, u_recv, n - 1)
     sums = u_recv[...].reshape(n * HEADS, slab)
     top = sums.astype(BF16)
@@ -337,16 +384,13 @@
         e_send[g, :, :slab] = embedded[g:g + 1, :]
         e_send[g, :, slab:] = jnp.broadcast_to(code, (1, 128))
 
-    def post(t, carry):
-        other = lax.rem(me + t, total)
-        g = other % n
+    def post(o, g):
         pltpu.make_async_remote_copy(
             src_ref=e_send.at[g], dst_ref=e_recv.at[me], send_sem=a2a_send.at[5],
-            recv_sem=a2a_recv.at[5], device_id=(other // n, g), device_id_type=MESH,
+            recv_sem=a2a_recv.at[5], device_id=(o, g), device_id_type=MESH,
         ).start()
-        return carry
-
-    lax.fori_loop(1, total, post, 0)
+
+    everyone(post)
     e_recv[me] = e_send[f]
     arrived(5, e_recv, total - 1)
 
@@ -436,6 +480,7 @@
             pltpu.SemaphoreType.DMA((10,)),
             pltpu.SemaphoreType.DMA((6,)),
             pltpu.SemaphoreType.DMA((6,)),
+            pltpu.SemaphoreType.REGULAR(((n_dp - 1).bit_length() + (n - 1).bit_length(),)),
         ] + [pieces] * 13,
         compiler_params=pltpu.CompilerParams(
             collective_id=0, has_side_effects=True, vmem_limit_bytes=67043328

time: 68.8 us -> 62.4 us (0.907)
  Pallas kernels: 66.5 us -> 60.1 us
    pallas_call x1, Pallas kernels: 66.5 us -> 60.1 us  [local(): pl.pallas_call(functools.partial(kernel, n_dp, n, chunks), out_shape=jax....]
where the time goes in v2:
time: 62.4 us; the launch traced here: 62.1 us
  Pallas kernels  60.1 us (96%)
  local copies, waits for them, and re-layouts  1.33 us (2%)
  between operations  0.66 us (1%)
    pallas_call x1, Pallas kernels, local(): pl.pallas_call(functools.partial(kernel, n_dp, n, chunks), out_shape=jax....  60.1 us
    unnamed x1, local copies, waits for them, and re-layouts  1.33 us

profile of v2, /device:TPU:0, one launch (start us, length us, event | category | flops | bytes accessed | tf_op | source)
XLA Modules:
  0.0 62.1 jit_solution(1097957108156620725)
XLA Ops:
  0.7 60.1 %shard_map.118 = bf16[1,4,4,512]{3,2,1,0:T(4,128)(2,1)} custom-call(s32[1]{0:T(128)S(6)} %copy.14.lengths, s32[8]{0:T(128)} %list_ids.1, s32[1,256]{1,0:T(1,128)} %bitcast.5, bf16[1,256,4096]{2,1,0:T(8,128)(2,1)} %hidden_hbm.1, f32[1,4096]{1,0:T(1,128)} %bitcast.3, f32[1,4096]{1,0:T(1,128)} %bitcast.4, f32[256,128]{1,0:T(8,128)} %constant.4.clone.cos_hbm, ...), custom_call_target="tpu_custom_call" | custom-call | tf_op jit(solution)/shard_map/pallas_call | solution.py:447
  60.8 1.3 %copy.15 = bf16[1,4,4,512]{3,2,1,0:T(4,128)(2,1)} copy(bf16[1,4,4,512]{3,2,1,0:T(4,128)(2,1)} %shard_map.118) | data formatting | bytes 32768
